TPU v7x, 32 devices: a whole 2x2x4 slice. The times are simulated.
32 devices in a mesh: space: 16 (over z, y, core), tm: 2 (over x).
Axes of the slice: x: 2, y: 2, z: 4, core: 2. Of those that a mesh axis runs over, the one named last changes fastest.
Arguments:
- row_orbitals: bfloat16 [8192, 2048], P('space', 'tm'), may hold values from -0.890625 to 0.890625
- column_orbitals: bfloat16 [256, 2048], P('space', 'tm'), may hold values from -0.890625 to 0.890625
- occupation: int32 [2048], replicated, may hold values from 0 to 2
- order: int32 [2048], replicated, may hold values from 0 to 2047, each once
- levels: float32 [2048], replicated, may hold values from 0.1 to 1
- times: float32 [2], replicated, may hold values from 0.05 to 1.5
- quad_weights: float32 [2], replicated, may hold values from 0.5 to 1.5
- freqs: float32 [8], replicated, may hold values from 0.1 to 4
Outputs:
- spectrum: float32 [8, 8192, 256], P(None, ('space', 'tm'))
Inputs may be any that keep to these rules, and one draw needn't show every extreme that they name: `order`: each index of 0 to 2047 once.
All inputs are finite; a program needn't handle non-finite values.
Results may differ from a plain program's by a relative error of at most 0.0026.
Values may be sent and summed in bfloat16 or wider, within the bound.
No kernel may reach another device: no remote copies, remote signals or barrier semaphores. Data moves between devices by JAX's collectives and lax.ppermute only.
A program may use at most 64 MiB of HBM per device.

v0:
```python
import jax
import jax.numpy as jnp
from jax import lax
from jax.sharding import PartitionSpec as P


def body(row_orbitals, column_orbitals, occupation, order, levels, times, quad_weights, freqs):
    energy = jnp.take(levels, order)
    filled = occupation.astype(jnp.float32) * 0.5
    rows_full = lax.all_to_all(row_orbitals, "tm", split_axis=0, concat_axis=1, tiled=True)
    decays = jnp.exp(-times[:, None] * energy[None, :])
    full_weight = filled[None, :] * decays
    empty_weight = (1.0 - filled)[None, :] * decays
    row_values = rows_full.astype(jnp.float32)[None]
    scaled_full = (row_values * full_weight[:, None, :]).astype(jnp.bfloat16)
    scaled_empty = (row_values * empty_weight[:, None, :]).astype(jnp.bfloat16)
    orbital_count = rows_full.shape[1]
    half_rows = scaled_full.shape[0] * scaled_full.shape[1]
    stacked = jnp.concatenate(
        (
            scaled_full.reshape(half_rows, orbital_count),
            scaled_empty.reshape(half_rows, orbital_count),
        ),
        axis=0,
    )
    col_count = column_orbitals.shape[0] * lax.axis_size("space")
    columns = lax.all_gather(column_orbitals, "tm", axis=1, tiled=True)
    greens = lax.dot_general(
        stacked,
        lax.all_gather(columns, "space", axis=0, tiled=True),
        (((1,), (1,)), ((), ())),
        preferred_element_type=jnp.float32,
    )
    product = (greens[:half_rows] * greens[half_rows:]).astype(jnp.bfloat16)
    time_count = times.shape[0]
    gathered = product.reshape(time_count, half_rows // time_count, col_count)
    sub_rows = gathered.shape[1]
    cosines = quad_weights[None, :] * jnp.cos(freqs[:, None] * times[None, :])
    spectrum = jnp.dot(
        cosines,
        gathered.reshape(time_count, sub_rows * col_count).astype(jnp.float32),
        precision=lax.Precision.HIGHEST,
    )
    return spectrum.reshape(freqs.shape[0], sub_rows, col_count)


def solution(mesh):
    placed = (P("space", "tm"), P("space", "tm"), P(), P(), P(), P(), P(), P())
    return jax.shard_map(
        body, mesh=mesh, in_specs=placed, out_specs=P(None, ("space", "tm"), None), check_vma=False
    )
```

profile of v0, /device:TPU:0, one launch (start us, length us, event | category | flops | bytes accessed | tf_op | source)
XLA Modules:
  0.0 66.5 jit_solution(772920246954484222)
XLA Ops:
  6.5 0.0 copy-start
  6.5 0.0 copy-start.1
  6.5 0.0 all-gather.2.cloned.1.call-start
  6.5 7.3 %all_gather.6 = bf16[16,2048]{1,0:T(8,128)(2,1)} all-gather(bf16[16,1024]{1,0:T(8,128)(2,1)} %param.9), channel_id=1, replica_groups=mesh['space'=16,'tm'=2] {'tm'}, dimensions={1}, use_global_device_ids=true | all-gather | bytes 98304 | tf_op jit(solution)/shard_map/all_gather | solution.py:27
  13.9 0.0 all-gather.2.cloned.1.call-update
  13.9 3.6 %all-to-all-start = ((bf16[2,256,1024]{2,1,0:T(8,128)(2,1)}), bf16[2,256,1024]{2,1,0:T(8,128)(2,1)S(1)}, u32[]{:S(2)}, u32[]{:S(2)}) async-start(bf16[2,256,1024]{2,1,0:T(8,128)(2,1)} %bitcast.18), calls=%async_computation | async-start | bytes 2097152 | tf_op jit(solution)/shard_map/all_to_all | solution.py:10
  17.5 0.0 copy-done.1
  17.5 0.0 copy-done
  17.5 0.0 copy-start.2
  17.5 0.0 copy-start.3
  17.5 11.8 %gather_fusion = f32[2048]{0:T(1024)S(1)} fusion(f32[2048]{0:T(1024)S(1)} %copy-done, s32[2048]{0:T(1024)S(1)} %fusion.7), kind=kCustom, calls=%fused_computation | custom fusion | bytes 24576 | tf_op jit(solution)/shard_map/jit(_take)/gather | solution.py:8
  29.3 0.0 copy-done.2
  29.4 0.0 copy-done.3
  29.4 0.1 fusion.6
  29.5 1.0 %all-to-all-done = bf16[2,256,1024]{2,1,0:T(8,128)(2,1)S(1)} async-done(((bf16[2,256,1024]{2,1,0:T(8,128)(2,1)}), bf16[2,256,1024]{2,1,0:T(8,128)(2,1)S(1)}, u32[]{:S(2)}, u32[]{:S(2)}) %all-to-all-start) | async-done | bytes 1048608 | tf_op jit(solution)/shard_map/all_to_all | solution.py:10
  30.5 0.2 convert_bitcast_fusion
  30.7 1.8 %copy.12 = f32[256,2,1024]{0,2,1:T(8,128)} copy(f32[256,2,1024]{2,0,1:T(8,128)S(1)} %convert_bitcast_fusion) | data formatting | bytes 4194304 | tf_op jit(solution)/shard_map/convert_element_type | solution.py:14
  32.5 1.9 %copy.13 = f32[256,2048]{1,0:T(8,128)S(1)} copy(f32[256,2048]{0,1:T(8,128)} %bitcast.14) | data formatting | bytes 4194304 | tf_op jit(solution)/shard_map/convert_element_type | solution.py:14
  34.4 3.1 %multiply_convert_fusion.1 = (bf16[2,256,2048]{2,1,0:T(8,128)(2,1)}, bf16[2,256,2048]{2,1,0:T(8,128)(2,1)}) fusion(f32[2,2048]{1,0:T(2,128)S(1)} %get-tuple-element.7, f32[256,2048]{1,0:T(8,128)S(1)} %copy.13, f32[2,2048]{1,0:T(2,128)S(1)} %get-tuple-element.8), kind=kLoop, calls=%fused_computation.6 | loop fusion | flops 4194304 | bytes 6324224 | tf_op jit(solution)/shard_map/convert_element_type | solution.py:15
  37.5 14.8 %all-gather.2.cloned.1.call-done = bf16[256,2048]{1,0:T(8,128)(2,1)} async-done(((bf16[16,2048]{1,0:T(8,128)(2,1)}), bf16[256,2048]{1,0:T(8,128)(2,1)}) %all-gather.2.cloned.1.call-update) | async-done | bytes 1048592 | tf_op jit(solution)/shard_map/all_gather | solution.py:30
  52.3 0.0 copy-start.4
  52.3 0.0 copy-start.5
  52.3 3.8 %fusion = f32[1024,256]{1,0:T(8,128)S(1)} fusion(bf16[256,2048]{1,0:T(8,128)(2,1)} %all-gather.2.cloned.1.call-done, bf16[512,2048]{1,0:T(8,128)(2,1)} %bitcast.16, bf16[512,2048]{1,0:T(8,128)(2,1)} %bitcast.15), kind=kOutput, calls=%fused_computation.1 | convolution fusion | flops 1082130432 | bytes 6291456 | tf_op jit(solution)/shard_map/dot_general | solution.py:28
  56.2 0.1 fusion.4
  56.2 0.1 reshape_reshape.3
  56.3 0.0 copy-done.4
  56.3 0.0 copy-done.5
  56.3 1.3 %fusion.8 = f32[8,256,256]{2,0,1:T(8,128)S(1)} fusion(bf16[256,256,2]{1,2,0:T(2,128)(2,1)S(1)} %bitcast.17, f32[8]{0:T(128)S(1)} %copy-done.4, f32[2]{0:T(128)S(1)} %copy-done.5, f32[2]{0:T(128)S(1)} %copy-done.3), kind=kOutput, calls=%fused_computation.18 | convolution fusion | flops 12582944 | bytes 2359344 | tf_op jit(solution)/shard_map/dot_general | solution.py:39
  57.7 2.0 %copy.14 = f32[8,256,256]{2,1,0:T(8,128)} copy(f32[8,256,256]{2,0,1:T(8,128)S(1)} %fusion.8) | data formatting | bytes 4194304 | tf_op jit(solution)/shard_map/dot_general | solution.py:39
  (3 shorter events, 0.0 us)
Async XLA Ops:
  6.5 11.0 %copy-start = (f32[2048]{0:T(1024)S(1)}, f32[2048]{0:T(1024)}, u32[]{:S(2)}) copy-start(f32[2048]{0:T(1024)} %param.12) | copy-start | bytes 24580
  6.5 10.9 %copy-start.1 = (s32[2048]{0:T(1024)S(1)}, s32[2048]{0:T(1024)}, u32[]{:S(2)}) copy-start(s32[2048]{0:T(1024)} %param.11) | copy-start | bytes 24580
  6.5 45.8 %all-gather.2.cloned.1.call-start = ((), (), s32[]{:S(2)}) async-start(), calls=%async_computation.1 | async-start | bytes 1114112 | tf_op jit(solution)/shard_map/all_gather | solution.py:30
  13.9 16.6 %all-to-all-start = ((bf16[2,256,1024]{2,1,0:T(8,128)(2,1)}), bf16[2,256,1024]{2,1,0:T(8,128)(2,1)S(1)}, u32[]{:S(2)}, u32[]{:S(2)}) async-start(bf16[2,256,1024]{2,1,0:T(8,128)(2,1)} %bitcast.18), calls=%async_computation | async-start | bytes 2097152 | tf_op jit(solution)/shard_map/all_to_all | solution.py:10
  17.5 11.8 %copy-start.2 = (s32[2048]{0:T(1024)S(1)}, s32[2048]{0:T(1024)}, u32[]{:S(2)}) copy-start(s32[2048]{0:T(1024)} %param.10) | copy-start | bytes 24580
  17.5 11.8 %copy-start.3 = (f32[2]{0:T(128)S(1)}, f32[2]{0:T(128)}, u32[]{:S(2)}) copy-start(f32[2]{0:T(128)} %param.13) | copy-start | bytes 28
  52.3 4.0 %copy-start.4 = (f32[8]{0:T(128)S(1)}, f32[8]{0:T(128)}, u32[]{:S(2)}) copy-start(f32[8]{0:T(128)} %param.15) | copy-start | bytes 100
  52.3 4.0 %copy-start.5 = (f32[2]{0:T(128)S(1)}, f32[2]{0:T(128)}, u32[]{:S(2)}) copy-start(f32[2]{0:T(128)} %param.14) | copy-start | bytes 28
Sparse Core Ops, SparseCore 0:
  14.0 38.2 all-gather.1
where the time goes:
time: 66.8 us; the launch traced here: 66.5 us
  local copies, waits for them, and re-layouts  17.6 us (26%)
  waiting for transfers between devices  15.8 us (24%)
  between operations  13.5 us (20%)
  blocking collectives  7.31 us (11%)
  matrix products  5.14 us (8%)
  starting transfers between devices  3.6 us (5%)
  other arithmetic  3.46 us (5%)
    all_gather x1, waiting for transfers between devices, body(): lax.all_gather(columns, 'space', axis=0, tiled=True)  14.8 us
    gather x1, local copies, waits for them, and re-layouts, body(): energy = jnp.take(levels, order)  11.8 us
    all_gather x1, blocking collectives, body(): columns = lax.all_gather(column_orbitals, 'tm', axis=1, tiled=True)  7.31 us
    dot_general x1, matrix products, body(): lax.dot_general(stacked, lax.all_gather(columns, 'space', axis=0, tiled=T...  3.8 us
    convert_element_type x2, local copies, waits for them, and re-layouts, body(): row_values = rows_full.astype(jnp.float32)[None]  3.73 us
    all_to_all x1, starting transfers between devices, body(): lax.all_to_all(row_orbitals, 'tm', split_axis=0, concat_axis=1, tiled=True)  3.59 us
    convert_element_type x1, other arithmetic, body(): scaled_full = (row_values * full_weight[:, None, :]).astype(jnp.bfloat16)  3.07 us
    dot_general x1, local copies, waits for them, and re-layouts, body(): jnp.dot(cosines, gathered.reshape(time_count, sub_rows * col_count).astyp...  1.96 us
  transfers between devices with their start and end apart: 2, of which 2 were waited for; matrix products, arithmetic and copies ran while one was open for 28% of the time, Pallas kernels for 0%

commit v1 on v0

--- a/solution.py
+++ b/solution.py
@@ -24,7 +24,8 @@
         axis=0,
     )
     col_count = column_orbitals.shape[0] * lax.axis_size("space")
-    columns = lax.all_gather(column_orbitals, "tm", axis=1, tiled=True)
+    found_now = lax.all_gather(column_orbitals, "tm")
+    columns = jnp.concatenate(found_now, axis=1)
     greens = lax.dot_general(
         stacked,
         lax.all_gather(columns, "space", axis=0, tiled=True),

time: 66.8 us -> 67.3 us (level)
  blocking collectives: 7.31 us -> 5.91 us
  waiting for transfers between devices: 15.8 us -> 17.1 us
  local copies, waits for them, and re-layouts: 17.6 us -> 18.3 us
    all_gather x1, blocking collectives: 7.31 us -> 5.91 us  [body(): found_now = lax.all_gather(column_orbitals, 'tm')]
    all_gather x1, waiting for transfers between devices: 14.8 us -> 16.1 us  [body(): lax.all_gather(columns, 'space', axis=0, tiled=True)]
where the time goes in v1:
time: 67.3 us; the launch traced here: 67.1 us
  local copies, waits for them, and re-layouts  18.3 us (27%)
  waiting for transfers between devices  17.1 us (25%)
  between operations  13.5 us (20%)
  blocking collectives  5.91 us (9%)
  matrix products  5.14 us (8%)
  starting transfers between devices  3.6 us (5%)
  other arithmetic  3.46 us (5%)
    all_gather x1, waiting for transfers between devices, body(): lax.all_gather(columns, 'space', axis=0, tiled=True)  16.1 us
    gather x1, local copies, waits for them, and re-layouts, body(): energy = jnp.take(levels, order)  11.8 us
    all_gather x1, blocking collectives, body(): found_now = lax.all_gather(column_orbitals, 'tm')  5.91 us
    dot_general x1, matrix products, body(): lax.dot_general(stacked, lax.all_gather(columns, 'space', axis=0, tiled=T...  3.8 us
    convert_element_type x2, local copies, waits for them, and re-layouts, body(): row_values = rows_full.astype(jnp.float32)[None]  3.73 us
    all_to_all x1, starting transfers between devices, body(): lax.all_to_all(row_orbitals, 'tm', split_axis=0, concat_axis=1, tiled=True)  3.59 us
    convert_element_type x1, other arithmetic, body(): scaled_full = (row_values * full_weight[:, None, :]).astype(jnp.bfloat16)  3.07 us
    dot_general x1, local copies, waits for them, and re-layouts, body(): jnp.dot(cosines, gathered.reshape(time_count, sub_rows * col_count).astyp...  1.96 us
  transfers between devices with their start and end apart: 2, of which 2 were waited for; matrix products, arithmetic and copies ran while one was open for 28% of the time, Pallas kernels for 0%

profile of v1, /device:TPU:0, one launch (start us, length us, event | category | flops | bytes accessed | tf_op | source)
XLA Modules:
  0.0 67.1 jit_solution(7302509247222079370)
XLA Ops:
  6.5 0.0 copy-start
  6.5 0.0 copy-start.1
  6.5 0.0 all-gather.3.cloned.1.call-start
  6.5 5.9 %all-gather = bf16[32,1024]{1,0:T(8,128)(2,1)S(1)} all-gather(bf16[16,1024]{1,0:T(8,128)(2,1)} %param.9), channel_id=2, replica_groups=mesh['space'=16,'tm'=2] {'tm'}, dimensions={0}, use_global_device_ids=true | all-gather | bytes 98304 | tf_op jit(solution)/shard_map/all_gather | solution.py:27
  12.5 0.1 copy.15
  12.5 0.6 copy.17
  13.2 0.0 all-gather.3.cloned.1.call-update
  13.2 3.6 %all-to-all-start = ((bf16[2,256,1024]{2,1,0:T(8,128)(2,1)}), bf16[2,256,1024]{2,1,0:T(8,128)(2,1)S(1)}, u32[]{:S(2)}, u32[]{:S(2)}) async-start(bf16[2,256,1024]{2,1,0:T(8,128)(2,1)} %bitcast.22), calls=%async_computation | async-start | bytes 2097152 | tf_op jit(solution)/shard_map/all_to_all | solution.py:10
  16.8 0.0 copy-done.1
  16.8 0.0 copy-done
  16.8 0.0 copy-start.2
  16.8 0.0 copy-start.3
  16.8 11.8 %gather_fusion = f32[2048]{0:T(1024)S(1)} fusion(f32[2048]{0:T(1024)S(1)} %copy-done, s32[2048]{0:T(1024)S(1)} %fusion.7), kind=kCustom, calls=%fused_computation | custom fusion | bytes 24576 | tf_op jit(solution)/shard_map/jit(_take)/gather | solution.py:8
  28.6 0.0 copy-done.2
  28.7 0.0 copy-done.3
  28.7 0.1 fusion.6
  28.8 1.0 %all-to-all-done = bf16[2,256,1024]{2,1,0:T(8,128)(2,1)S(1)} async-done(((bf16[2,256,1024]{2,1,0:T(8,128)(2,1)}), bf16[2,256,1024]{2,1,0:T(8,128)(2,1)S(1)}, u32[]{:S(2)}, u32[]{:S(2)}) %all-to-all-start) | async-done | bytes 1048608 | tf_op jit(solution)/shard_map/all_to_all | solution.py:10
  29.8 0.2 convert_bitcast_fusion
  30.0 1.8 %copy.13 = f32[256,2,1024]{0,2,1:T(8,128)} copy(f32[256,2,1024]{2,0,1:T(8,128)S(1)} %convert_bitcast_fusion) | data formatting | bytes 4194304 | tf_op jit(solution)/shard_map/convert_element_type | solution.py:14
  31.8 1.9 %copy.14 = f32[256,2048]{1,0:T(8,128)S(1)} copy(f32[256,2048]{0,1:T(8,128)} %bitcast.18) | data formatting | bytes 4194304 | tf_op jit(solution)/shard_map/convert_element_type | solution.py:14
  33.8 3.1 %multiply_convert_fusion.1 = (bf16[2,256,2048]{2,1,0:T(8,128)(2,1)}, bf16[2,256,2048]{2,1,0:T(8,128)(2,1)}) fusion(f32[2,2048]{1,0:T(2,128)S(1)} %get-tuple-element.7, f32[256,2048]{1,0:T(8,128)S(1)} %copy.14, f32[2,2048]{1,0:T(2,128)S(1)} %get-tuple-element.8), kind=kLoop, calls=%fused_computation.6 | loop fusion | flops 4194304 | bytes 6324224 | tf_op jit(solution)/shard_map/convert_element_type | solution.py:15
  36.8 16.1 %all-gather.3.cloned.1.call-done = bf16[256,2048]{1,0:T(8,128)(2,1)} async-done(((bf16[16,2048]{1,0:T(8,128)(2,1)}), bf16[256,2048]{1,0:T(8,128)(2,1)}) %all-gather.3.cloned.1.call-update) | async-done | bytes 1048592 | tf_op jit(solution)/shard_map/all_gather | solution.py:31
  52.9 0.0 copy-start.4
  52.9 0.0 copy-start.5
  52.9 3.8 %fusion = f32[1024,256]{1,0:T(8,128)S(1)} fusion(bf16[256,2048]{1,0:T(8,128)(2,1)} %all-gather.3.cloned.1.call-done, bf16[512,2048]{1,0:T(8,128)(2,1)} %bitcast.20, bf16[512,2048]{1,0:T(8,128)(2,1)} %bitcast.19), kind=kOutput, calls=%fused_computation.1 | convolution fusion | flops 1082130432 | bytes 6291456 | tf_op jit(solution)/shard_map/dot_general | solution.py:29
  56.8 0.1 fusion.4
  56.8 0.1 reshape_reshape.3
  56.9 0.0 copy-done.4
  56.9 0.0 copy-done.5
  56.9 1.3 %fusion.8 = f32[8,256,256]{2,0,1:T(8,128)S(1)} fusion(bf16[256,256,2]{1,2,0:T(2,128)(2,1)S(1)} %bitcast.21, f32[8]{0:T(128)S(1)} %copy-done.4, f32[2]{0:T(128)S(1)} %copy-done.5, f32[2]{0:T(128)S(1)} %copy-done.3), kind=kOutput, calls=%fused_computation.18 | convolution fusion | flops 12582944 | bytes 2359344 | tf_op jit(solution)/shard_map/dot_general | solution.py:40
  58.3 2.0 %copy.16 = f32[8,256,256]{2,1,0:T(8,128)} copy(f32[8,256,256]{2,0,1:T(8,128)S(1)} %fusion.8) | data formatting | bytes 4194304 | tf_op jit(solution)/shard_map/dot_general | solution.py:40
  (3 shorter events, 0.0 us)
Async XLA Ops:
  6.5 10.3 %copy-start = (f32[2048]{0:T(1024)S(1)}, f32[2048]{0:T(1024)}, u32[]{:S(2)}) copy-start(f32[2048]{0:T(1024)} %param.12) | copy-start | bytes 24580
  6.5 10.2 %copy-start.1 = (s32[2048]{0:T(1024)S(1)}, s32[2048]{0:T(1024)}, u32[]{:S(2)}) copy-start(s32[2048]{0:T(1024)} %param.11) | copy-start | bytes 24580
  6.5 46.4 %all-gather.3.cloned.1.call-start = ((), (), s32[]{:S(2)}) async-start(), calls=%async_computation.1 | async-start | bytes 1114112 | tf_op jit(solution)/shard_map/all_gather | solution.py:31
  13.2 16.6 %all-to-all-start = ((bf16[2,256,1024]{2,1,0:T(8,128)(2,1)}), bf16[2,256,1024]{2,1,0:T(8,128)(2,1)S(1)}, u32[]{:S(2)}, u32[]{:S(2)}) async-start(bf16[2,256,1024]{2,1,0:T(8,128)(2,1)} %bitcast.22), calls=%async_computation | async-start | bytes 2097152 | tf_op jit(solution)/shard_map/all_to_all | solution.py:10
  16.8 11.8 %copy-start.2 = (s32[2048]{0:T(1024)S(1)}, s32[2048]{0:T(1024)}, u32[]{:S(2)}) copy-start(s32[2048]{0:T(1024)} %param.10) | copy-start | bytes 24580
  16.8 11.8 %copy-start.3 = (f32[2]{0:T(128)S(1)}, f32[2]{0:T(128)}, u32[]{:S(2)}) copy-start(f32[2]{0:T(128)} %param.13) | copy-start | bytes 28
  52.9 3.9 %copy-start.4 = (f32[8]{0:T(128)S(1)}, f32[8]{0:T(128)}, u32[]{:S(2)}) copy-start(f32[8]{0:T(128)} %param.15) | copy-start | bytes 100
  52.9 4.0 %copy-start.5 = (f32[2]{0:T(128)S(1)}, f32[2]{0:T(128)}, u32[]{:S(2)}) copy-start(f32[2]{0:T(128)} %param.14) | copy-start | bytes 28
Sparse Core Ops, SparseCore 0:
  13.3 39.5 all-gather.2
